TPU v7x, 32 devices: a whole 2x2x4 slice. The times are simulated.
32 devices in a mesh: epoch: 4 (over y, x), blend: 8 (over z, core).
Axes of the slice: x: 2, y: 2, z: 4, core: 2. Of those that a mesh axis runs over, the one named last changes fastest.
Arguments:
- visit_flux: bfloat16 [16, 32, 6, 16384], P('epoch', None, None, 'blend'), may hold values from -6 to 6
- visit_precision: bfloat16 [16, 32, 6, 16384], P('epoch', None, None, 'blend'), may hold values from 0.25 to 4
- visit_live: int32 [16, 32], P('epoch'), may hold values 0 or 1
- footprint: int32 [32, 8, 16384], P('blend', None, 'epoch'), may hold values 0 or 1
- source_count: int32 [32], P('blend'), may hold values from 1 to 8
- spectra_init: float32 [32, 8, 6], P('blend'), may hold values from 0.2 to 1.2
- morphology_init: float32 [32, 8, 16384], P('blend', None, 'epoch'), may hold values from 0 to 0.25
Outputs:
- coadd_flux: float32 [32, 6, 16384], P('blend', None, 'epoch')
- spectra: float32 [32, 8, 6], P('blend')
- morphology: float32 [32, 8, 16384], P('blend', None, 'epoch')
All inputs are finite; a program needn't handle non-finite values. No bound on the sum of `visit_live` or of `footprint` on one device may be relied on, other than what follows from the above.
Results may differ from a plain program's by a relative error of at most 0.0003.
Values sent between devices are 32-bit elements; how exact they have to be, the bound alone decides.
A program may use at most 64 MiB of HBM per device.

v0:
```python
import jax
import jax.numpy as jnp
from jax import lax
from jax.sharding import PartitionSpec as P

ITERS = 2


def on_device(
    visit_flux, visit_precision, visit_live, footprint, source_count, spectra_init, morphology_init
):
    weights = visit_precision.astype(jnp.float32) * visit_live.astype(jnp.float32)[:, :, None, None]
    numerator = jnp.sum(weights * visit_flux.astype(jnp.float32), axis=0)
    weight_sum = jnp.sum(weights, axis=0)
    pix_part = morphology_init.shape[2]
    owned = morphology_init.shape[0]
    numerator, weight_sum = (
        lax.psum_scatter(numerator, "epoch", scatter_dimension=2, tiled=True),
        lax.psum_scatter(weight_sum, "epoch", scatter_dimension=2, tiled=True),
    )
    every_blend, band_count, piece = numerator.shape
    numerator = numerator.reshape(every_blend, band_count, 1, piece)
    weight_sum = weight_sum.reshape(every_blend, band_count, 1, piece)
    numerator, weight_sum = (
        lax.all_to_all(numerator, "blend", split_axis=0, concat_axis=2, tiled=True),
        lax.all_to_all(weight_sum, "blend", split_axis=0, concat_axis=2, tiled=True),
    )
    blocks = numerator.shape[2]
    numerator = numerator.reshape(owned, band_count, blocks, 1, piece)
    weight_sum = weight_sum.reshape(owned, band_count, blocks, 1, piece)
    numerator, weight_sum = (
        lax.all_to_all(numerator, "epoch", split_axis=2, concat_axis=3, tiled=True),
        lax.all_to_all(weight_sum, "epoch", split_axis=2, concat_axis=3, tiled=True),
    )
    numerator = numerator.reshape(owned, band_count, pix_part)
    weight_sum = weight_sum.reshape(owned, band_count, pix_part)
    coadd_flux = numerator / (1.0 + weight_sum)
    coverage = weight_sum / (1.0 + weight_sum)
    slots = footprint.shape[1]
    source_live = (jnp.arange(slots, dtype=jnp.int32)[None, :] < source_count[:, None]).astype(
        jnp.float32
    )
    footprint_mask = footprint.astype(jnp.float32) * source_live[:, :, None]
    live_count = source_count.astype(jnp.float32)
    morphology = morphology_init * footprint_mask
    spectra = spectra_init
    highest = lax.Precision.HIGHEST
    for iteration in range(ITERS):
        blend_model = jnp.einsum("bkc,bkp->bcp", spectra, morphology, precision=highest)
        residual = coverage * (coadd_flux - blend_model)
        morph_grad = jnp.einsum("bkc,bcp->bkp", spectra, residual, precision=highest)
        morph_step = 1.0 / (1.0 + live_count[:, None] * jnp.sum(spectra * spectra, axis=2))
        morphology = (
            jnp.maximum(0.0, morphology + morph_grad * morph_step[:, :, None]) * footprint_mask
        )
        blend_model = jnp.einsum("bkc,bkp->bcp", spectra, morphology, precision=highest)
        residual = coverage * (coadd_flux - blend_model)
        spectra_grad = jnp.einsum("bkp,bcp->bkc", morphology, residual, precision=highest)
        morph_norm = jnp.sum(morphology * morphology, axis=2)
        spectra_grad, morph_norm = lax.psum((spectra_grad, morph_norm), "epoch")
        spectra = jnp.maximum(
            0.0, spectra + spectra_grad / (1.0 + live_count[:, None] * morph_norm)[:, :, None]
        )
    return (coadd_flux, spectra, morphology)


def solution(mesh):
    in_specs = (
        P("epoch", None, None, "blend"),
        P("epoch", None, None, "blend"),
        P("epoch", None),
        P("blend", None, "epoch"),
        P("blend"),
        P("blend", None, None),
        P("blend", None, "epoch"),
    )
    out_specs = (P("blend", None, "epoch"), P("blend", None, None), P("blend", None, "epoch"))
    return jax.shard_map(
        on_device, mesh=mesh, in_specs=in_specs, out_specs=out_specs, check_vma=False
    )
```

profile of v0, /device:TPU:0, one launch (start us, length us, event | category | flops | bytes accessed | tf_op | source)
XLA Modules:
  0.0 167.4 jit_solution(2619093483653560001)
XLA Ops:
  7.2 0.0 reduce-scatter.5.cloned.1.call-start
  7.2 0.7 convert_element_type.23
  7.9 6.4 %fusion = (f32[32,6,2048]{2,0,1:T(8,128)}, f32[32,6,2048]{2,0,1:T(8,128)}) fusion(bf16[4,32,6,2048]{3,1,2,0:T(8,128)(2,1)} %param.8, f32[4,32]{1,0:T(4,128)S(1)} %convert_element_type.23, bf16[4,32,6,2048]{3,1,2,0:T(8,128)(2,1)} %param.7), kind=kLoop, calls=%fused_computation.2 | loop fusion | flops 8650752 | bytes 9437696 | tf_op jit(solution)/shard_map/reduce_sum | solution.py:14
  14.3 0.0 reduce-scatter.5.cloned.1.call-update
  14.3 0.0 reduce-scatter.3.cloned.1.call-start
  14.4 0.0 copy-start.4
  14.4 0.0 copy-start.3
  14.4 0.7 reduce-scatter.3.cloned.1.call-update
  15.1 33.3 %reduce-scatter.5.cloned.1.call-done = f32[32,6,512]{2,0,1:T(8,128)} async-done(((f32[32,6,2048]{2,0,1:T(8,128)}), f32[32,6,512]{2,0,1:T(8,128)}) %reduce-scatter.5.cloned.1.call-update) | async-done | bytes 393232 | tf_op jit(solution)/shard_map/reduce_scatter | solution.py:19
  48.4 2.1 %copy.58 = f32[32,6,1,512]{3,2,1,0:T(1,128)} copy(f32[32,6,1,512]{3,0,1,2:T(8,128)} %bitcast.57) | data formatting | bytes 786432 | tf_op jit(solution)/shard_map/reshape | solution.py:23
  50.5 4.6 %all-to-all-start.2 = ((f32[32,6,1,512]{3,2,1,0:T(1,128)}), f32[32,6,1,512]{3,2,1,0:T(1,128)S(1)}, u32[]{:S(2)}, u32[]{:S(2)}) async-start(f32[32,6,1,512]{3,2,1,0:T(1,128)} %copy.58), calls=%async_computation.4 | async-start | bytes 786432 | tf_op jit(solution)/shard_map/all_to_all | solution.py:26
  55.1 27.4 %reduce-scatter.3.cloned.1.call-done = f32[32,6,512]{2,0,1:T(8,128)} async-done(((f32[32,6,2048]{2,0,1:T(8,128)}), f32[32,6,512]{2,0,1:T(8,128)}) %reduce-scatter.3.cloned.1.call-update) | async-done | bytes 393232 | tf_op jit(solution)/shard_map/reduce_scatter | solution.py:18
  82.5 2.1 %copy.54 = f32[32,6,1,512]{3,2,1,0:T(1,128)} copy(f32[32,6,1,512]{3,0,1,2:T(8,128)} %bitcast.58) | data formatting | bytes 786432 | tf_op jit(solution)/shard_map/reshape | solution.py:22
  84.7 0.0 all-to-all-done.2
  84.7 4.6 %all-to-all-start = ((f32[32,6,1,512]{3,2,1,0:T(1,128)}), f32[32,6,1,512]{3,2,1,0:T(1,128)S(1)}, u32[]{:S(2)}, u32[]{:S(2)}) async-start(f32[32,6,1,512]{3,2,1,0:T(1,128)} %copy.54), calls=%async_computation.1 | async-start | bytes 786432 | tf_op jit(solution)/shard_map/all_to_all | solution.py:25
  89.3 0.8 copy.85
  90.1 11.7 %all-to-all-done = f32[32,6,1,512]{3,2,1,0:T(1,128)S(1)} async-done(((f32[32,6,1,512]{3,2,1,0:T(1,128)}), f32[32,6,1,512]{3,2,1,0:T(1,128)S(1)}, u32[]{:S(2)}, u32[]{:S(2)}) %all-to-all-start) | async-done | bytes 393248 | tf_op jit(solution)/shard_map/all_to_all | solution.py:25
  101.8 3.5 %all-to-all-start.3 = ((f32[4,6,8,1,512]{4,0,1,3,2:T(4,128)}), f32[4,6,8,1,512]{4,0,1,3,2:T(4,128)S(1)}, u32[]{:S(2)}, u32[]{:S(2)}) async-start(f32[4,6,8,1,512]{4,0,1,3,2:T(4,128)} %bitcast.51), calls=%async_computation.5 | async-start | bytes 786432 | tf_op jit(solution)/shard_map/all_to_all | solution.py:33
  105.2 0.0 copy-done.4
  105.3 0.0 copy-done.3
  105.3 0.1 copy.68
  105.4 0.1 fusion.19
  105.4 0.8 copy.86
  106.3 5.2 %all-to-all-done.3 = f32[4,6,8,1,512]{4,0,1,3,2:T(4,128)S(1)} async-done(((f32[4,6,8,1,512]{4,0,1,3,2:T(4,128)}), f32[4,6,8,1,512]{4,0,1,3,2:T(4,128)S(1)}, u32[]{:S(2)}, u32[]{:S(2)}) %all-to-all-start.3) | async-done | bytes 393248 | tf_op jit(solution)/shard_map/all_to_all | solution.py:33
  111.5 3.5 %all-to-all-start.1 = ((f32[4,6,8,1,512]{4,0,1,3,2:T(4,128)}), f32[4,6,8,1,512]{4,0,1,3,2:T(4,128)S(1)}, u32[]{:S(2)}, u32[]{:S(2)}) async-start(f32[4,6,8,1,512]{4,0,1,3,2:T(4,128)} %bitcast.52), calls=%async_computation.2 | async-start | bytes 786432 | tf_op jit(solution)/shard_map/all_to_all | solution.py:32
  115.0 0.1 add_divide_fusion.3
  115.1 0.3 copy.77
  115.4 0.0 copy-start
  115.4 0.0 copy-start.2
  115.4 0.3 reshape.92
  115.7 5.1 %all-to-all-done.1 = f32[4,6,8,1,512]{4,0,1,3,2:T(4,128)S(1)} async-done(((f32[4,6,8,1,512]{4,0,1,3,2:T(4,128)}), f32[4,6,8,1,512]{4,0,1,3,2:T(4,128)S(1)}, u32[]{:S(2)}, u32[]{:S(2)}) %all-to-all-start.1) | async-done | bytes 393248 | tf_op jit(solution)/shard_map/all_to_all | solution.py:32
  120.9 0.3 copy.75
  121.1 0.3 reshape.91
  121.4 0.1 add_divide_fusion.1
  121.5 1.0 copy.71
  122.5 0.0 copy-done
  122.5 0.0 copy-done.2
  122.5 0.7 fusion.13
  123.2 0.8 multiply_reduce_fusion.2
  124.0 0.6 fusion.11
  124.6 1.2 fusion.20
  125.7 15.3 %all-reduce.1 = (f32[4,8,6]{2,1,0:T(8,128)S(1)}, f32[4,8]{1,0:T(4,128)S(1)}) all-reduce(f32[4,8,6]{2,1,0:T(8,128)S(1)} %fusion.20, f32[4,8]{1,0:T(4,128)S(1)} %get-tuple-element.26), channel_id=1, replica_groups=mesh['epoch'=4,'blend'=8] {'epoch'}, use_global_device_ids=true, to_apply=%region_5.0 | all-reduce | flops 224 | bytes 1792 | tf_op jit(solution)/shard_map/psum | solution.py:60
  141.1 0.1 multiply_add_fusion.1
  141.2 0.2 multiply_reduce_fusion.3
  141.3 0.7 fusion.3
  142.0 0.1 add_divide_fusion.2
  142.1 0.8 multiply_reduce_fusion.1
  142.8 0.0 copy-start.1
  142.8 0.7 fusion.1
  143.5 1.2 fusion.21
  144.7 15.1 %all-reduce = (f32[4,8,6]{2,1,0:T(8,128)S(1)}, f32[4,8]{1,0:T(4,128)S(1)}) all-reduce(f32[4,8,6]{2,1,0:T(8,128)S(1)} %fusion.21, f32[4,8]{1,0:T(4,128)S(1)} %get-tuple-element.28), channel_id=1, replica_groups=mesh['epoch'=4,'blend'=8] {'epoch'}, use_global_device_ids=true, to_apply=%region_9.0 | all-reduce | flops 224 | bytes 1792 | tf_op jit(solution)/shard_map/psum | solution.py:60
  159.7 0.1 multiply_add_fusion
  159.8 0.1 add_maximum_fusion
  159.9 0.7 copy.72
  160.6 0.0 copy-done.1
  (4 shorter events, 0.1 us)
Async XLA Ops:
  7.2 41.2 %reduce-scatter.5.cloned.1.call-start = ((), (), s32[]{:S(2)}) async-start(), calls=%async_computation.7 | async-start | bytes 1966080 | tf_op jit(solution)/shard_map/reduce_scatter | solution.py:19
  14.3 68.2 %reduce-scatter.3.cloned.1.call-start = ((), (), s32[]{:S(2)}) async-start(), calls=%async_computation.6 | async-start | bytes 1966080 | tf_op jit(solution)/shard_map/reduce_scatter | solution.py:18
  14.4 90.9 %copy-start.4 = (s32[4]{0:T(128)S(1)}, s32[4]{0:T(128)}, u32[]{:S(2)}) copy-start(s32[4]{0:T(128)} %param.11) | copy-start | bytes 52
  14.4 90.9 %copy-start.3 = (f32[4,8,6]{1,0,2:T(4,128)S(1)}, f32[4,8,6]{1,0,2:T(4,128)}, u32[]{:S(2)}) copy-start(f32[4,8,6]{1,0,2:T(4,128)} %param.12) | copy-start | bytes 2308
  50.5 34.1 %all-to-all-start.2 = ((f32[32,6,1,512]{3,2,1,0:T(1,128)}), f32[32,6,1,512]{3,2,1,0:T(1,128)S(1)}, u32[]{:S(2)}, u32[]{:S(2)}) async-start(f32[32,6,1,512]{3,2,1,0:T(1,128)} %copy.58), calls=%async_computation.4 | async-start | bytes 786432 | tf_op jit(solution)/shard_map/all_to_all | solution.py:26
  84.7 17.1 %all-to-all-start = ((f32[32,6,1,512]{3,2,1,0:T(1,128)}), f32[32,6,1,512]{3,2,1,0:T(1,128)S(1)}, u32[]{:S(2)}, u32[]{:S(2)}) async-start(f32[32,6,1,512]{3,2,1,0:T(1,128)} %copy.54), calls=%async_computation.1 | async-start | bytes 786432 | tf_op jit(solution)/shard_map/all_to_all | solution.py:25
  101.8 9.7 %all-to-all-start.3 = ((f32[4,6,8,1,512]{4,0,1,3,2:T(4,128)}), f32[4,6,8,1,512]{4,0,1,3,2:T(4,128)S(1)}, u32[]{:S(2)}, u32[]{:S(2)}) async-start(f32[4,6,8,1,512]{4,0,1,3,2:T(4,128)} %bitcast.51), calls=%async_computation.5 | async-start | bytes 786432 | tf_op jit(solution)/shard_map/all_to_all | solution.py:33
  111.5 9.3 %all-to-all-start.1 = ((f32[4,6,8,1,512]{4,0,1,3,2:T(4,128)}), f32[4,6,8,1,512]{4,0,1,3,2:T(4,128)S(1)}, u32[]{:S(2)}, u32[]{:S(2)}) async-start(f32[4,6,8,1,512]{4,0,1,3,2:T(4,128)} %bitcast.52), calls=%async_computation.2 | async-start | bytes 786432 | tf_op jit(solution)/shard_map/all_to_all | solution.py:32
  115.4 7.1 %copy-start = (s32[4,8,4096]{2,1,0:T(8,128)S(1)}, s32[4,8,4096]{2,1,0:T(8,128)}, u32[]{:S(2)}) copy-start(s32[4,8,4096]{2,1,0:T(8,128)} %param.10) | copy-start | bytes 1572868
  115.4 7.1 %copy-start.2 = (f32[4,8,4096]{2,1,0:T(8,128)S(1)}, f32[4,8,4096]{2,1,0:T(8,128)}, u32[]{:S(2)}) copy-start(f32[4,8,4096]{2,1,0:T(8,128)} %param.13) | copy-start | bytes 1572868
  142.8 17.7 %copy-start.1 = (f32[4,8,4096]{2,1,0:T(8,128)}, f32[4,8,4096]{2,1,0:T(8,128)S(1)}, u32[]{:S(2)}) copy-start(f32[4,8,4096]{2,1,0:T(8,128)S(1)} %get-tuple-element.29) | copy-start | bytes 1572868
Sparse Core Ops, SparseCore 0:
  14.5 33.8 reduce-scatter.4
  51.4 31.1 reduce-scatter.2
where the time goes:
time: 168 us; the launch traced here: 167 us
  waiting for transfers between devices  83.4 us (50%)
  blocking collectives  30.4 us (18%)
  starting transfers between devices  16.2 us (10%)
  between operations  14.2 us (8%)
  local copies, waits for them, and re-layouts  8.92 us (5%)
  other arithmetic  7.82 us (5%)
  matrix products  6.48 us (4%)
    reduce_scatter x1, waiting for transfers between devices, on_device(): lax.psum_scatter(weight_sum, 'epoch', scatter_dimension=2, tiled=True)  33.3 us
    psum x2, blocking collectives, on_device(): spectra_grad, morph_norm = lax.psum((spectra_grad, morph_norm), 'epoch')  30.4 us
    reduce_scatter x1, waiting for transfers between devices, on_device(): lax.psum_scatter(numerator, 'epoch', scatter_dimension=2, tiled=True)  27.4 us
    all_to_all x1, waiting for transfers between devices, on_device(): lax.all_to_all(numerator, 'blend', split_axis=0, concat_axis=2, tiled=True)  11.7 us
    reduce_sum x1, other arithmetic, on_device(): weight_sum = jnp.sum(weights, axis=0)  6.42 us
    all_to_all x1, waiting for transfers between devices, on_device(): lax.all_to_all(weight_sum, 'epoch', split_axis=2, concat_axis=3, tiled=True)  5.22 us
    all_to_all x1, waiting for transfers between devices, on_device(): lax.all_to_all(numerator, 'epoch', split_axis=2, concat_axis=3, tiled=True)  5.14 us
    all_to_all x1, starting transfers between devices, on_device(): lax.all_to_all(weight_sum, 'blend', split_axis=0, concat_axis=2, tiled=True)  4.59 us
  transfers between devices with their start and end apart: 6, of which 5 were waited for; matrix products, arithmetic and copies ran while one was open for 4% of the time, Pallas kernels for 0%

commit v1 on v0

--- a/solution.py
+++ b/solution.py
@@ -30,7 +30,15 @@
     weight_sum = weight_sum.reshape(owned, band_count, blocks, 1, piece)
     numerator, weight_sum = (
         lax.all_to_all(numerator, "epoch", split_axis=2, concat_axis=3, tiled=True),
-        lax.all_to_all(weight_sum, "epoch", split_axis=2, concat_axis=3, tiled=True),
+        jnp.concatenate(
+            lax.all_to_all(
+                jnp.stack(jnp.split(weight_sum, lax.axis_size("epoch"), axis=2), axis=0),
+                axis_name="epoch",
+                split_axis=0,
+                concat_axis=0,
+            ),
+            3,
+        ),
     )
     numerator = numerator.reshape(owned, band_count, pix_part)
     weight_sum = weight_sum.reshape(owned, band_count, pix_part)

time: 168 us -> 168 us (level)
  no operation moved by 1% of the time
where the time goes in v1:
time: 168 us; the launch traced here: 167 us
  waiting for transfers between devices  82.8 us (49%)
  blocking collectives  30.4 us (18%)
  starting transfers between devices  16.2 us (10%)
  between operations  14.2 us (8%)
  other arithmetic  8.74 us (5%)
  local copies, waits for them, and re-layouts  8.64 us (5%)
  matrix products  6.48 us (4%)
    reduce_scatter x1, waiting for transfers between devices, on_device(): lax.psum_scatter(weight_sum, 'epoch', scatter_dimension=2, tiled=True)  33.3 us
    psum x2, blocking collectives, on_device(): spectra_grad, morph_norm = lax.psum((spectra_grad, morph_norm), 'epoch')  30.4 us
    reduce_scatter x1, waiting for transfers between devices, on_device(): lax.psum_scatter(numerator, 'epoch', scatter_dimension=2, tiled=True)  27.4 us
    all_to_all x1, waiting for transfers between devices, on_device(): lax.all_to_all(numerator, 'blend', split_axis=0, concat_axis=2, tiled=True)  11 us
    reduce_sum x1, other arithmetic, on_device(): weight_sum = jnp.sum(weights, axis=0)  6.42 us
    all_to_all x1, waiting for transfers between devices, on_device(): lax.all_to_all(jnp.stack(jnp.split(weight_sum, lax.axis_size('epoch'), ax...  5.22 us
    all_to_all x1, waiting for transfers between devices, on_device(): lax.all_to_all(numerator, 'epoch', split_axis=2, concat_axis=3, tiled=True)  5.18 us
    all_to_all x1, starting transfers between devices, on_device(): lax.all_to_all(weight_sum, 'blend', split_axis=0, concat_axis=2, tiled=True)  4.59 us
  transfers between devices with their start and end apart: 6, of which 5 were waited for; matrix products, arithmetic and copies ran while one was open for 4% of the time, Pallas kernels for 0%

profile of v1, /device:TPU:0, one launch (start us, length us, event | category | flops | bytes accessed | tf_op | source)
XLA Modules:
  0.0 167.5 jit_solution(4045377614913481731)
XLA Ops:
  7.2 0.0 reduce-scatter.5.cloned.1.call-start
  7.2 0.7 convert_element_type.23
  7.9 6.4 %fusion = (f32[32,6,2048]{2,0,1:T(8,128)}, f32[32,6,2048]{2,0,1:T(8,128)}) fusion(bf16[4,32,6,2048]{3,1,2,0:T(8,128)(2,1)} %param.8, f32[4,32]{1,0:T(4,128)S(1)} %convert_element_type.23, bf16[4,32,6,2048]{3,1,2,0:T(8,128)(2,1)} %param.7), kind=kLoop, calls=%fused_computation.2 | loop fusion | flops 8650752 | bytes 9437696 | tf_op jit(solution)/shard_map/reduce_sum | solution.py:14
  14.3 0.0 reduce-scatter.5.cloned.1.call-update
  14.3 0.0 reduce-scatter.3.cloned.1.call-start
  14.4 0.7 reduce-scatter.3.cloned.1.call-update
  15.1 33.3 %reduce-scatter.5.cloned.1.call-done = f32[32,6,512]{2,0,1:T(8,128)} async-done(((f32[32,6,2048]{2,0,1:T(8,128)}), f32[32,6,512]{2,0,1:T(8,128)}) %reduce-scatter.5.cloned.1.call-update) | async-done | bytes 393232 | tf_op jit(solution)/shard_map/reduce_scatter | solution.py:19
  48.4 0.0 copy-start.4
  48.4 0.0 copy-start.3
  48.4 2.2 %copy.129 = f32[32,6,1,512]{3,2,1,0:T(1,128)} copy(f32[32,6,1,512]{3,0,2,1:T(8,128)} %bitcast.62) | data formatting | bytes 786432 | tf_op jit(solution)/shard_map/reshape | solution.py:23
  50.5 4.6 %all-to-all-start.2 = ((f32[32,6,1,512]{3,2,1,0:T(1,128)}), f32[32,6,1,512]{3,2,1,0:T(1,128)S(1)}, u32[]{:S(2)}, u32[]{:S(2)}) async-start(f32[32,6,1,512]{3,2,1,0:T(1,128)} %copy.129), calls=%async_computation.4 | async-start | bytes 786432 | tf_op jit(solution)/shard_map/all_to_all | solution.py:26
  55.1 27.4 %reduce-scatter.3.cloned.1.call-done = f32[32,6,512]{2,0,1:T(8,128)} async-done(((f32[32,6,2048]{2,0,1:T(8,128)}), f32[32,6,512]{2,0,1:T(8,128)}) %reduce-scatter.3.cloned.1.call-update) | async-done | bytes 393232 | tf_op jit(solution)/shard_map/reduce_scatter | solution.py:18
  82.5 2.1 %copy.125 = f32[32,6,1,512]{3,2,1,0:T(1,128)} copy(f32[32,6,1,512]{3,0,1,2:T(8,128)} %bitcast.63) | data formatting | bytes 786432 | tf_op jit(solution)/shard_map/reshape | solution.py:22
  84.7 0.0 all-to-all-done.2
  84.7 4.6 %all-to-all-start = ((f32[32,6,1,512]{3,2,1,0:T(1,128)}), f32[32,6,1,512]{3,2,1,0:T(1,128)S(1)}, u32[]{:S(2)}, u32[]{:S(2)}) async-start(f32[32,6,1,512]{3,2,1,0:T(1,128)} %copy.125), calls=%async_computation.1 | async-start | bytes 786432 | tf_op jit(solution)/shard_map/all_to_all | solution.py:25
  89.3 0.3 fusion.20
  89.5 0.2 copy_bitcast_fusion.3
  89.7 0.2 copy_bitcast_fusion.1
  89.9 0.9 pad_maximum_fusion
  90.8 11.0 %all-to-all-done = f32[32,6,1,512]{3,2,1,0:T(1,128)S(1)} async-done(((f32[32,6,1,512]{3,2,1,0:T(1,128)}), f32[32,6,1,512]{3,2,1,0:T(1,128)S(1)}, u32[]{:S(2)}, u32[]{:S(2)}) %all-to-all-start) | async-done | bytes 393248 | tf_op jit(solution)/shard_map/all_to_all | solution.py:25
  101.8 3.5 %all-to-all-start.3 = ((f32[4,4,6,2,1,512]{5,3,2,1,4,0:T(2,128)}), f32[4,4,6,2,1,512]{5,3,2,1,4,0:T(2,128)S(1)}, u32[]{:S(2)}, u32[]{:S(2)}) async-start(f32[4,4,6,2,1,512]{5,3,2,1,4,0:T(2,128)} %pad_maximum_fusion), calls=%async_computation.5 | async-start | bytes 786432 | tf_op jit(solution)/shard_map/all_to_all | solution.py:34
  105.2 0.0 copy-done.4
  105.3 0.0 copy-done.3
  105.3 0.1 copy.141
  105.4 0.1 fusion.19
  105.4 0.8 copy.161
  106.3 5.2 %all-to-all-done.3 = f32[4,4,6,2,1,512]{5,3,2,1,4,0:T(2,128)S(1)} async-done(((f32[4,4,6,2,1,512]{5,3,2,1,4,0:T(2,128)}), f32[4,4,6,2,1,512]{5,3,2,1,4,0:T(2,128)S(1)}, u32[]{:S(2)}, u32[]{:S(2)}) %all-to-all-start.3) | async-done | bytes 393248 | tf_op jit(solution)/shard_map/all_to_all | solution.py:34
  111.5 3.5 %all-to-all-start.1 = ((f32[4,6,8,1,512]{4,0,1,3,2:T(4,128)}), f32[4,6,8,1,512]{4,0,1,3,2:T(4,128)S(1)}, u32[]{:S(2)}, u32[]{:S(2)}) async-start(f32[4,6,8,1,512]{4,0,1,3,2:T(4,128)} %bitcast.57), calls=%async_computation.2 | async-start | bytes 786432 | tf_op jit(solution)/shard_map/all_to_all | solution.py:32
  115.0 0.1 add_divide_fusion.3
  115.1 0.3 copy.150
  115.3 0.0 copy-start
  115.4 0.0 copy-start.2
  115.4 0.3 reshape.91
  115.6 5.2 %all-to-all-done.1 = f32[4,6,8,1,512]{4,0,1,3,2:T(4,128)S(1)} async-done(((f32[4,6,8,1,512]{4,0,1,3,2:T(4,128)}), f32[4,6,8,1,512]{4,0,1,3,2:T(4,128)S(1)}, u32[]{:S(2)}, u32[]{:S(2)}) %all-to-all-start.1) | async-done | bytes 393248 | tf_op jit(solution)/shard_map/all_to_all | solution.py:32
  120.9 0.3 copy.148
  121.1 0.3 reshape.90
  121.4 0.1 add_divide_fusion.1
  121.5 1.0 copy.144
  122.5 0.0 copy-done
  122.5 0.0 copy-done.2
  122.5 0.7 fusion.13
  123.2 0.8 multiply_reduce_fusion.2
  124.0 0.6 fusion.11
  124.6 1.2 fusion.21
  125.7 15.4 %all-reduce.1 = (f32[4,8,6]{2,1,0:T(8,128)S(1)}, f32[4,8]{1,0:T(4,128)S(1)}) all-reduce(f32[4,8,6]{2,1,0:T(8,128)S(1)} %fusion.21, f32[4,8]{1,0:T(4,128)S(1)} %get-tuple-element.39), channel_id=1, replica_groups=mesh['epoch'=4,'blend'=8] {'epoch'}, use_global_device_ids=true, to_apply=%region_5.0 | all-reduce | flops 224 | bytes 1792 | tf_op jit(solution)/shard_map/psum | solution.py:68
  141.1 0.1 multiply_add_fusion.1
  141.2 0.2 multiply_reduce_fusion.3
  141.4 0.7 fusion.3
  142.0 0.1 add_divide_fusion.2
  142.1 0.8 multiply_reduce_fusion.1
  142.9 0.0 copy-start.1
  142.9 0.7 fusion.1
  143.6 1.2 fusion.22
  144.7 15.1 %all-reduce = (f32[4,8,6]{2,1,0:T(8,128)S(1)}, f32[4,8]{1,0:T(4,128)S(1)}) all-reduce(f32[4,8,6]{2,1,0:T(8,128)S(1)} %fusion.22, f32[4,8]{1,0:T(4,128)S(1)} %get-tuple-element.41), channel_id=1, replica_groups=mesh['epoch'=4,'blend'=8] {'epoch'}, use_global_device_ids=true, to_apply=%region_9.0 | all-reduce | flops 224 | bytes 1792 | tf_op jit(solution)/shard_map/psum | solution.py:68
  159.8 0.1 multiply_add_fusion
  159.8 0.1 add_maximum_fusion
  159.9 0.7 copy.145
  160.6 0.0 copy-done.1
  (3 shorter events, 0.0 us)
Async XLA Ops:
  7.2 41.2 %reduce-scatter.5.cloned.1.call-start = ((), (), s32[]{:S(2)}) async-start(), calls=%async_computation.7 | async-start | bytes 1966080 | tf_op jit(solution)/shard_map/reduce_scatter | solution.py:19
  14.3 68.2 %reduce-scatter.3.cloned.1.call-start = ((), (), s32[]{:S(2)}) async-start(), calls=%async_computation.6 | async-start | bytes 1966080 | tf_op jit(solution)/shard_map/reduce_scatter | solution.py:18
  48.4 56.9 %copy-start.4 = (s32[4]{0:T(128)S(1)}, s32[4]{0:T(128)}, u32[]{:S(2)}) copy-start(s32[4]{0:T(128)} %param.11) | copy-start | bytes 52
  48.4 56.9 %copy-start.3 = (f32[4,8,6]{1,0,2:T(4,128)S(1)}, f32[4,8,6]{1,0,2:T(4,128)}, u32[]{:S(2)}) copy-start(f32[4,8,6]{1,0,2:T(4,128)} %param.12) | copy-start | bytes 2308
  50.5 34.1 %all-to-all-start.2 = ((f32[32,6,1,512]{3,2,1,0:T(1,128)}), f32[32,6,1,512]{3,2,1,0:T(1,128)S(1)}, u32[]{:S(2)}, u32[]{:S(2)}) async-start(f32[32,6,1,512]{3,2,1,0:T(1,128)} %copy.129), calls=%async_computation.4 | async-start | bytes 786432 | tf_op jit(solution)/shard_map/all_to_all | solution.py:26
  84.7 17.1 %all-to-all-start = ((f32[32,6,1,512]{3,2,1,0:T(1,128)}), f32[32,6,1,512]{3,2,1,0:T(1,128)S(1)}, u32[]{:S(2)}, u32[]{:S(2)}) async-start(f32[32,6,1,512]{3,2,1,0:T(1,128)} %copy.125), calls=%async_computation.1 | async-start | bytes 786432 | tf_op jit(solution)/shard_map/all_to_all | solution.py:25
  101.8 9.7 %all-to-all-start.3 = ((f32[4,4,6,2,1,512]{5,3,2,1,4,0:T(2,128)}), f32[4,4,6,2,1,512]{5,3,2,1,4,0:T(2,128)S(1)}, u32[]{:S(2)}, u32[]{:S(2)}) async-start(f32[4,4,6,2,1,512]{5,3,2,1,4,0:T(2,128)} %pad_maximum_fusion), calls=%async_computation.5 | async-start | bytes 786432 | tf_op jit(solution)/shard_map/all_to_all | solution.py:34
  111.5 9.3 %all-to-all-start.1 = ((f32[4,6,8,1,512]{4,0,1,3,2:T(4,128)}), f32[4,6,8,1,512]{4,0,1,3,2:T(4,128)S(1)}, u32[]{:S(2)}, u32[]{:S(2)}) async-start(f32[4,6,8,1,512]{4,0,1,3,2:T(4,128)} %bitcast.57), calls=%async_computation.2 | async-start | bytes 786432 | tf_op jit(solution)/shard_map/all_to_all | solution.py:32
  115.3 7.2 %copy-start = (s32[4,8,4096]{2,1,0:T(8,128)S(1)}, s32[4,8,4096]{2,1,0:T(8,128)}, u32[]{:S(2)}) copy-start(s32[4,8,4096]{2,1,0:T(8,128)} %param.10) | copy-start | bytes 1572868
  115.4 7.1 %copy-start.2 = (f32[4,8,4096]{2,1,0:T(8,128)S(1)}, f32[4,8,4096]{2,1,0:T(8,128)}, u32[]{:S(2)}) copy-start(f32[4,8,4096]{2,1,0:T(8,128)} %param.13) | copy-start | bytes 1572868
  142.9 17.8 %copy-start.1 = (f32[4,8,4096]{2,1,0:T(8,128)}, f32[4,8,4096]{2,1,0:T(8,128)S(1)}, u32[]{:S(2)}) copy-start(f32[4,8,4096]{2,1,0:T(8,128)S(1)} %get-tuple-element.42) | copy-start | bytes 1572868
Sparse Core Ops, SparseCore 0:
  14.5 33.8 reduce-scatter.4
  51.4 31.1 reduce-scatter.2
